TPU v7x, 32 devices: a whole 2x2x4 slice. The times are simulated.
32 devices in a mesh: dop: 2 (over core), tm: 16 (over z, y, x).
Axes of the slice: x: 2, y: 2, z: 4, core: 2. Of those that a mesh axis runs over, the one named last changes fastest.
Arguments:
- surveillance: bfloat16 [2, 16, 8192], P(None, 'tm', 'dop'), may hold values from -6 to 6
- reference_signal: bfloat16 [2, 16, 8192], P(None, 'tm', 'dop'), may hold values from -6 to 6
Outputs:
- ambiguity: float32 [2048, 2, 512], P('tm', None, 'dop')
All inputs are finite; a program needn't handle non-finite values.
Results may differ from a plain program's by a relative error of at most 0.0029.
Values may be sent and summed in bfloat16 or wider, within the bound.
No kernel may reach another device: no remote copies, remote signals or barrier semaphores. Data moves between devices by JAX's collectives and lax.ppermute only.
A program may use at most 128 MiB of HBM per device.

v0:
```python
import math

import jax
import jax.numpy as jnp
from jax import lax
from jax.sharding import PartitionSpec as P

F = 512
LAGS = 2048
BLOCK = 8192


def from_behind(value, axis, steps):
    count = lax.axis_size(axis)
    first, last = (max(0, -steps), min(count, count - steps))
    return lax.ppermute(value, axis, [(source, source + steps) for source in range(first, last)])


def toeplitz_rows(segment, height, breadth):
    length = height + breadth - 1
    repeated = jnp.tile(segment, (1, height + 1))[:, : height * (length + 1)]
    return repeated.reshape(2, height, length + 1)[:, :, :breadth]


def mix_rows(samples, sample_index, doppler, window):
    phase_step = jnp.mod(doppler[:, None] * sample_index[None, :], window)
    phase_angle = phase_step.astype(jnp.float32) * (2.0 * math.pi / window)
    cosine = jnp.cos(phase_angle)
    sine_part = jnp.sin(phase_angle)
    real_in = samples[0].astype(jnp.float32)[None, :]
    imag_in = samples[1].astype(jnp.float32)[None, :]
    mixed_real = (real_in * cosine + imag_in * sine_part).astype(jnp.bfloat16)
    mixed_imag = (imag_in * cosine - real_in * sine_part).astype(jnp.bfloat16)
    upper_half = jnp.concatenate([mixed_real, mixed_imag], 1)
    lower_half = jnp.concatenate([mixed_imag, -mixed_real], 1)
    return jnp.concatenate([upper_half, lower_half], 0)


def lag_product(toeplitz, mixed):
    height = toeplitz.shape[1]
    stacked = toeplitz.reshape(2 * height, toeplitz.shape[2])
    return lax.dot_general(
        stacked, mixed, (((0,), (1,)), ((), ())), preferred_element_type=jnp.float32
    )


def on_device(surveillance, reference_signal):
    pieces = surveillance.shape[2]
    blocks_here = surveillance.shape[1]
    time_devices = lax.axis_size("tm")
    window = BLOCK * blocks_here * time_devices
    lag_rows = LAGS // time_devices
    full_block = lax.all_gather(reference_signal, "dop", axis=2, tiled=True)
    bin_count = F
    row_shift = lax.axis_index("dop") * pieces
    block_tail = full_block[:, -1, BLOCK - LAGS + 1 :]
    earlier = from_behind(block_tail, "tm", 1)
    earlier_tails = jnp.concatenate(
        [earlier[:, None, :], full_block[:, :-1, BLOCK - LAGS + 1 :]], 1
    )
    extended = jnp.concatenate([earlier_tails, full_block], 2)
    row_count = surveillance.shape[2]
    height = min(512, row_count)
    sub_count = row_count // height
    doppler = jnp.arange(bin_count, dtype=jnp.int32) - F // 2
    block_start = lax.axis_index("tm") * blocks_here

    def one_turn(turn_no, running):
        block_no = turn_no // sub_count
        inside = turn_no % sub_count * height
        offset = row_shift + inside
        ext_row = lax.dynamic_index_in_dim(extended, block_no, 1, keepdims=False)
        segment = lax.dynamic_slice_in_dim(
            ext_row, offset, height + lag_rows * lax.axis_size("tm") - 1, 1
        )[:, ::-1]
        toeplitz = toeplitz_rows(segment, height, lag_rows * lax.axis_size("tm"))
        signal_row = lax.dynamic_index_in_dim(surveillance, block_no, 1, keepdims=False)
        samples = lax.dynamic_slice_in_dim(signal_row, inside, height, 1)[:, ::-1]
        sample_index = (
            (block_start + block_no) * BLOCK
            + offset
            + height
            - 1
            - jnp.arange(height, dtype=jnp.int32)
        )
        return running + lag_product(toeplitz, mix_rows(samples, sample_index, doppler, window))

    partial_value = lax.psum_scatter(
        lax.fori_loop(
            0,
            blocks_here * sub_count,
            one_turn,
            jnp.zeros((lag_rows * lax.axis_size("tm"), 2 * bin_count), jnp.float32),
        ),
        "tm",
        scatter_dimension=0,
        tiled=True,
    )
    result = lax.psum_scatter(
        partial_value.reshape(lag_rows, 2, F), "dop", scatter_dimension=2, tiled=True
    )
    return result * (1.0 / math.sqrt(window))


def solution(mesh):
    return jax.shard_map(
        on_device,
        mesh=mesh,
        in_specs=(P(None, "tm", "dop"), P(None, "tm", "dop")),
        out_specs=P("tm", None, "dop"),
        check_vma=False,
    )
```

profile of v0, /device:TPU:0, one launch (start us, length us, event | category | flops | bytes accessed | tf_op | source)
XLA Modules:
  0.0 706.5 jit_solution(10309439441344766599)
XLA Ops:
  15.0 410.3 %while.19 = (s32[]{:T(128)}, f32[2048,1024]{1,0:T(8,128)}, s32[]{:T(128)}, bf16[2,1,10239]{2,0,1:T(2,128)(2,1)S(1)}, bf16[2,1,4096]{2,0,1:T(2,128)(2,1)}, /*inde...) while((s32[]{:T(128)}, f32[2048,1024]{1,0:T(8,128)}, ...), condition=%wide.region_1.2_spmd.clone, body=%wide.region_0.1_spmd.clone.sunk | while | flops 4318824448 | bytes 143802912 | solution.py:89
  30.8 12.7 %reshape.83 = bf16[2625534]{0:T(1024)(128)(2,1)} reshape(bf16[2,513,2559]{2,1,0:T(8,128)(2,1)} %tile.32) | data formatting | bytes 10502136 | tf_op jit(solution)/shard_map/while
  43.5 7.7 %tile.33 = bf16[2,1312767]{1,0:T(2,128)(2,1)} reshape(bf16[2625534]{0:T(1024)(128)(2,1)} %reshape.83) | data formatting | bytes 10502136 | tf_op jit(solution)/shard_map/while/body/eval_jaxpr/tile | solution.py:21
  82.1 12.7 %reshape.83 = bf16[2625534]{0:T(1024)(128)(2,1)} reshape(bf16[2,513,2559]{2,1,0:T(8,128)(2,1)} %tile.32) | data formatting | bytes 10502136 | tf_op jit(solution)/shard_map/while
  94.8 7.7 %tile.33 = bf16[2,1312767]{1,0:T(2,128)(2,1)} reshape(bf16[2625534]{0:T(1024)(128)(2,1)} %reshape.83) | data formatting | bytes 10502136 | tf_op jit(solution)/shard_map/while/body/eval_jaxpr/tile | solution.py:21
  133.4 12.7 %reshape.83 = bf16[2625534]{0:T(1024)(128)(2,1)} reshape(bf16[2,513,2559]{2,1,0:T(8,128)(2,1)} %tile.32) | data formatting | bytes 10502136 | tf_op jit(solution)/shard_map/while
  146.1 7.7 %tile.33 = bf16[2,1312767]{1,0:T(2,128)(2,1)} reshape(bf16[2625534]{0:T(1024)(128)(2,1)} %reshape.83) | data formatting | bytes 10502136 | tf_op jit(solution)/shard_map/while/body/eval_jaxpr/tile | solution.py:21
  158.9 6.8 select_add_fusion.2
  184.7 12.7 %reshape.83 = bf16[2625534]{0:T(1024)(128)(2,1)} reshape(bf16[2,513,2559]{2,1,0:T(8,128)(2,1)} %tile.32) | data formatting | bytes 10502136 | tf_op jit(solution)/shard_map/while
  197.4 7.7 %tile.33 = bf16[2,1312767]{1,0:T(2,128)(2,1)} reshape(bf16[2625534]{0:T(1024)(128)(2,1)} %reshape.83) | data formatting | bytes 10502136 | tf_op jit(solution)/shard_map/while/body/eval_jaxpr/tile | solution.py:21
  236.0 12.7 %reshape.83 = bf16[2625534]{0:T(1024)(128)(2,1)} reshape(bf16[2,513,2559]{2,1,0:T(8,128)(2,1)} %tile.32) | data formatting | bytes 10502136 | tf_op jit(solution)/shard_map/while
  248.6 7.7 %tile.33 = bf16[2,1312767]{1,0:T(2,128)(2,1)} reshape(bf16[2625534]{0:T(1024)(128)(2,1)} %reshape.83) | data formatting | bytes 10502136 | tf_op jit(solution)/shard_map/while/body/eval_jaxpr/tile | solution.py:21
  287.2 12.7 %reshape.83 = bf16[2625534]{0:T(1024)(128)(2,1)} reshape(bf16[2,513,2559]{2,1,0:T(8,128)(2,1)} %tile.32) | data formatting | bytes 10502136 | tf_op jit(solution)/shard_map/while
  299.9 7.7 %tile.33 = bf16[2,1312767]{1,0:T(2,128)(2,1)} reshape(bf16[2625534]{0:T(1024)(128)(2,1)} %reshape.83) | data formatting | bytes 10502136 | tf_op jit(solution)/shard_map/while/body/eval_jaxpr/tile | solution.py:21
  338.5 12.7 %reshape.83 = bf16[2625534]{0:T(1024)(128)(2,1)} reshape(bf16[2,513,2559]{2,1,0:T(8,128)(2,1)} %tile.32) | data formatting | bytes 10502136 | tf_op jit(solution)/shard_map/while
  351.2 7.7 %tile.33 = bf16[2,1312767]{1,0:T(2,128)(2,1)} reshape(bf16[2625534]{0:T(1024)(128)(2,1)} %reshape.83) | data formatting | bytes 10502136 | tf_op jit(solution)/shard_map/while/body/eval_jaxpr/tile | solution.py:21
  389.8 12.7 %reshape.83 = bf16[2625534]{0:T(1024)(128)(2,1)} reshape(bf16[2,513,2559]{2,1,0:T(8,128)(2,1)} %tile.32) | data formatting | bytes 10502136 | tf_op jit(solution)/shard_map/while
  402.5 7.7 %tile.33 = bf16[2,1312767]{1,0:T(2,128)(2,1)} reshape(bf16[2625534]{0:T(1024)(128)(2,1)} %reshape.83) | data formatting | bytes 10502136 | tf_op jit(solution)/shard_map/while/body/eval_jaxpr/tile | solution.py:21
  425.4 180.0 %reduce-scatter.5.cloned.1.call-done = f32[128,1024]{1,0:T(8,128)} async-done(((f32[2048,1024]{1,0:T(8,128)}), f32[128,1024]{1,0:T(8,128)}) %reduce-scatter.5.cloned.1.call-update) | async-done | bytes 524304 | tf_op jit(solution)/shard_map/reduce_scatter | solution.py:88
  606.9 26.2 %copy.5 = f32[128,2,512]{1,0,2:T(8,128)} copy(f32[128,2,512]{2,1,0:T(2,128)S(1)} %reshape.71) | data formatting | bytes 1048576
  633.1 24.6 %reshape.78 = f32[512,256]{1,0:T(8,128)} reshape(f32[512,128,2]{2,1,0:T(8,128)} %bitcast.40) | data formatting | bytes 1048576
  657.7 10.5 %reduce-scatter.7.cloned.1.call-done = f32[256,256]{1,0:T(8,128)} async-done(((f32[512,256]{1,0:T(8,128)}), f32[256,256]{1,0:T(8,128)}) %reduce-scatter.7.cloned.1.call-update) | async-done | bytes 262160
  668.2 18.8 %reshape.79 = f32[256,128,2]{2,1,0:T(8,128)} reshape(f32[256,256]{1,0:T(8,128)} %reduce-scatter.7.cloned.1.call-done) | data formatting | bytes 524288
  687.0 11.8 %copy.6 = f32[128,2,256]{2,1,0:T(2,128)S(1)} copy(f32[128,2,256]{1,0,2:T(8,128)} %bitcast.42) | data formatting | bytes 524288
  (203 shorter events, 251.1 us)
Async XLA Ops:
  6.5 598.8 %reduce-scatter.5.cloned.1.call-start = ((), (), s32[]{:S(2)}) async-start(), calls=%async_computation.2 | async-start | bytes 8912896 | tf_op jit(solution)/shard_map/reduce_scatter | solution.py:88
  8.8 6.1 collective-permute-start
  51.2 3.9 slice-start.1
  53.6 2.7 slice-start.2
  63.1 3.2 copy-start
  102.4 3.9 slice-start.1
  104.9 2.7 slice-start.2
  114.4 3.2 copy-start
  153.7 3.9 slice-start.1
  156.2 2.7 slice-start.2
  165.7 3.2 copy-start
  205.0 3.9 slice-start.1
  207.5 2.7 slice-start.2
  217.0 3.2 copy-start
  256.3 3.9 slice-start.1
  258.8 2.7 slice-start.2
  268.2 3.2 copy-start
  307.6 3.9 slice-start.1
  319.5 3.2 copy-start
  358.9 3.9 slice-start.1
  370.8 3.2 copy-start
  410.1 3.9 slice-start.1
  422.1 3.2 copy-start
  425.3 242.9 %reduce-scatter.7.cloned.1.call-start = ((), (), s32[]{:S(2)}) async-start(), calls=%async_computation.3 | async-start | bytes 786432
  (11 other events, 27.9 us)
Sparse Core Ops, SparseCore 0:
  425.5 179.8 reduce-scatter.4
  657.8 10.3 reduce-scatter.6
where the time goes:
time: 708 us; the launch traced here: 707 us
  local copies, waits for them, and re-layouts  363 us (51%)
  waiting for transfers between devices  192 us (27%)
  other arithmetic  76.4 us (11%)
  matrix products  54.3 us (8%)
  between operations  13.4 us (2%)
    reduce_scatter x1, waiting for transfers between devices, on_device(): lax.psum_scatter(lax.fori_loop(0, blocks_here * sub_count, one_turn, jnp....  180 us
    while x80, local copies, waits for them, and re-layouts  159 us
    another operation x16, local copies, waits for them, and re-layouts, toeplitz_rows(): repeated = jnp.tile(segment, (1, height + 1))[:, :height * (length + 1)]  83.4 us
    unnamed x4, local copies, waits for them, and re-layouts  81.4 us
    dot_general x8, matrix products, lag_product(): lax.dot_general(stacked, mixed, (((0,), (1,)), ((), ())), preferred_eleme...  54.3 us
    convert_element_type x8, other arithmetic, mix_rows(): mixed_real = (real_in * cosine + imag_in * sine_part).astype(jnp.bfloat16)  38 us
    neg x8, other arithmetic, mix_rows(): lower_half = jnp.concatenate([mixed_imag, -mixed_real], 1)  37.3 us
    slice x16, local copies, waits for them, and re-layouts, toeplitz_rows(): repeated = jnp.tile(segment, (1, height + 1))[:, :height * (length + 1)]  19.9 us
  transfers between devices with their start and end apart: 3, of which 3 were waited for; matrix products, arithmetic and copies ran while one was open for 0% of the time, Pallas kernels for 0%

commit v1 on v0

v1 whole, which is shorter than its diff:
```python
import functools
import math

import jax
import jax.numpy as jnp
import numpy as np
from jax import lax
from jax.experimental import pallas as pl
from jax.experimental.pallas import tpu as pltpu
from jax.sharding import PartitionSpec as P

F = 512
LAGS = 2048
LANES = 128


def unit(turns_num, turns_den):
    angle = 2.0 * np.pi * np.mod(turns_num, turns_den) / turns_den
    return np.cos(angle), np.sin(angle)


def body(pos_ref, g_ref, d_ref, mix_ref, kap_ref, tw_ref, place_ref, out_ref, s_ref, rp_ref, rx_ref, acc_ref,
         *, chunks, rows, groups, pad, lags, half, per_step):
    step = pl.program_id(0)

    @pl.when(step == 0)
    def _():
        acc_ref[...] = jnp.zeros_like(acc_ref)
        rp_ref[0:pad] = jnp.zeros((pad, 2, rows, LANES), jnp.float32)

        def first(c, _):
            sr = g_ref[c, 0].astype(jnp.float32)
            si = g_ref[c, 1].astype(jnp.float32)
            tr, ti = mix_ref[0], mix_ref[1]
            kr, ki = kap_ref[0, c], kap_ref[1, c]
            mr = tr * kr - ti * ki
            mi = tr * ki + ti * kr
            s_ref[c, 0] = sr * mr - si * mi
            s_ref[c, 1] = sr * mi + si * mr
            rp_ref[pad + c, 0] = g_ref[c, 2].astype(jnp.float32)
            rp_ref[pad + c, 1] = g_ref[c, 3].astype(jnp.float32)
            return 0

        lax.fori_loop(0, chunks, first, 0)
        lane = lax.broadcasted_iota(jnp.int32, (rows, LANES), 1)
        base = pos_ref[0]

        for grp in range(groups):
            shift = base + grp
            whole = shift // LANES
            part = shift - whole * LANES

            def second(c, _):
                at = c + pad - whole
                for ri in range(2):
                    cur = pltpu.roll(rp_ref[at, ri], part, 1)
                    prev = pltpu.roll(rp_ref[at - 1, ri], part, 1)
                    rx_ref[c, ri, grp * rows : (grp + 1) * rows, :] = jnp.where(lane >= part, cur, prev)
                return 0

            lax.fori_loop(0, chunks, second, 0)

    total = None
    for pair in range(chunks // 2):
        real_rows = []
        for inner in range(per_step):
            a = step * per_step + inner
            start = rows - 1 - a
            yr, yi = [], []
            for c in (2 * pair, 2 * pair + 1):
                rr = rx_ref[c, 0, pl.ds(start, lags), :]
                ri = rx_ref[c, 1, pl.ds(start, lags), :]
                sr = s_ref[c, 0, pl.ds(a, 1), :]
                si = s_ref[c, 1, pl.ds(a, 1), :]
                yr.append((sr * rr + si * ri).astype(jnp.bfloat16))
                yi.append((si * rr - sr * ri).astype(jnp.bfloat16))
            real_rows.append(jnp.concatenate(yr, 1))
            real_rows.append(jnp.concatenate(yi, 1))
        lhs = jnp.concatenate(real_rows, 0)
        term = jnp.dot(lhs, d_ref[pair], preferred_element_type=jnp.float32)
        total = term if total is None else total + term

    sums = [acc_ref[i] for i in range(4)]
    for inner in range(per_step):
        a = step * per_step + inner
        cosine = tw_ref[0, pl.ds(a, 1), :]
        sine = tw_ref[1, pl.ds(a, 1), :]
        for ri in range(2):
            z = total[(2 * inner + ri) * lags : (2 * inner + ri + 1) * lags]
            c, d = z[:, :half], z[:, half:]
            sums[2 * ri] = sums[2 * ri] + (c * cosine - d * sine)
            sums[2 * ri + 1] = sums[2 * ri + 1] + (d * cosine + c * sine)
    for i in range(4):
        acc_ref[i] = sums[i]

    @pl.when(step == pl.num_programs(0) - 1)
    def _():
        cr, dr, ci, di = sums
        put = functools.partial(
            jnp.dot, preferred_element_type=jnp.float32, precision=lax.Precision.HIGHEST
        )
        up, down = place_ref[0], place_ref[1]
        out_ref[:, 0, :] = put(cr + di, up) + put(cr - di, down)
        out_ref[:, 1, :] = put(ci - dr, up) + put(ci + dr, down)


def gather(value, tm, dop):
    return lax.all_gather(value, ("tm", "dop"), axis=0, tiled=False)


def on_device(surveillance, reference_signal):
    pieces = surveillance.shape[2]
    assert surveillance.shape[1] == 1
    tm, dop = lax.axis_size("tm"), lax.axis_size("dop")
    chunks = tm * dop
    window = pieces * chunks
    rows = pieces // LANES
    lags = LAGS // tm
    bins = F // dop
    half = max(bins // 2, LANES)
    groups = 1 + -(-(lags - 1) // rows)
    longest = (LAGS - lags) // rows + groups - 1
    pad = longest // LANES + 1
    per_step = min(4, rows)

    local = jnp.concatenate([surveillance, reference_signal], 0).reshape(4, LANES, rows).transpose(0, 2, 1)
    local = jnp.concatenate([local[:2], local[2:, ::-1]], 0)
    gathered = gather(local, tm, dop)

    half_bins = 2 * np.arange(bins // 2) + 1
    b = np.arange(chunks * LANES, dtype=np.int64)
    spread = np.zeros((chunks * LANES, 2, half))
    cosine, sine = unit(half_bins[None, :] * b[:, None], 2 * chunks * LANES)
    spread[:, 0, : bins // 2], spread[:, 1, : bins // 2] = cosine, sine
    spread = jnp.asarray(spread.reshape(chunks // 2, 2 * LANES, 2 * half), jnp.bfloat16)
    twiddle = np.zeros((2, rows, half), np.float32)
    cosine, sine = unit(half_bins[None, :] * np.arange(rows)[:, None], 2 * window)
    twiddle[0, :, : bins // 2], twiddle[1, :, : bins // 2] = cosine, sine
    twiddle = jnp.asarray(twiddle / math.sqrt(window))
    place = np.zeros((2, half, bins), np.float32)
    for j in range(bins // 2):
        place[0, j, bins // 2 + j] = 1.0
        place[1, j, bins // 2 - 1 - j] = 1.0
    centre = -F + 2 * bins * np.arange(dop) + bins - 1
    inside = np.arange(rows)[:, None] + rows * np.arange(LANES)[None, :]
    cosine, sine = unit(centre[:, None, None] * inside[None], 2 * window)
    mix = np.stack([cosine, -sine], 1).astype(np.float32)
    cosine, sine = unit(centre[:, None] * np.arange(chunks)[None, :], 2 * chunks)
    kappa = np.broadcast_to(np.stack([cosine, -sine], 1)[:, :, :, None, None], (dop, 2, chunks, 1, LANES))
    mine = lax.axis_index("dop")
    mix = lax.dynamic_index_in_dim(jnp.asarray(mix), mine, 0, keepdims=False)
    kappa = lax.dynamic_index_in_dim(jnp.asarray(kappa, jnp.float32), mine, 0, keepdims=False)
    first_shift = (lax.axis_index("tm") * (lags // rows)).astype(jnp.int32).reshape(1)

    vmem = pl.BlockSpec(memory_space=pltpu.VMEM)
    return pl.pallas_call(
        functools.partial(body, chunks=chunks, rows=rows, groups=groups, pad=pad, lags=lags, half=half,
                          per_step=per_step),
        out_shape=jax.ShapeDtypeStruct((lags, 2, bins), jnp.float32),
        grid=(rows // per_step,),
        in_specs=[pl.BlockSpec(memory_space=pltpu.SMEM)] + [vmem] * 6,
        out_specs=vmem,
        scratch_shapes=[
            pltpu.VMEM((chunks, 2, rows, LANES), jnp.float32),
            pltpu.VMEM((pad + chunks, 2, rows, LANES), jnp.float32),
            pltpu.VMEM((chunks, 2, groups * rows, LANES), jnp.float32),
            pltpu.VMEM((4, lags, half), jnp.float32),
        ],
        compiler_params=pltpu.CompilerParams(
            dimension_semantics=("arbitrary",), vmem_limit_bytes=60 * 2**20
        ),
    )(first_shift, gathered, spread, mix, kappa, twiddle, jnp.asarray(place))


def solution(mesh):
    return jax.shard_map(
        on_device,
        mesh=mesh,
        in_specs=(P(None, "tm", "dop"), P(None, "tm", "dop")),
        out_specs=P("tm", None, "dop"),
        check_vma=False,
    )
```

time: 708 us -> 115 us (0.16)
  local copies, waits for them, and re-layouts: 363 us -> 3.27 us
  waiting for transfers between devices: 192 us -> 55.3 us
  other arithmetic: 76.4 us -> 1.42 us
  matrix products: 54.3 us -> 0 us
  Pallas kernels: 0 us -> 40.8 us
    reduce_scatter x1 -> x0, waiting for transfers between devices: 180 us -> none  [on_device(): lax.psum_scatter(lax.fori_loop(0, blocks_here * sub_count, one_turn, jnp....]
    while x80 -> x0, local copies, waits for them, and re-layouts: 159 us -> none
    another operation x16 -> x0, local copies, waits for them, and re-layouts: 83.4 us -> none  [toeplitz_rows(): repeated = jnp.tile(segment, (1, height + 1))[:, :height * (length + 1)]]
    unnamed x4 -> x0, local copies, waits for them, and re-layouts: 81.4 us -> none
    all_gather x0 -> x1, waiting for transfers between devices: none -> 55.3 us  [gather(): return lax.all_gather(value, ('tm', 'dop'), axis=0, tiled=False)]
    dot_general x8 -> x0, matrix products: 54.3 us -> none  [lag_product(): lax.dot_general(stacked, mixed, (((0,), (1,)), ((), ())), preferred_eleme...]
    pallas_call x0 -> x1, Pallas kernels: none -> 40.8 us  [on_device(): pl.pallas_call(functools.partial(body, chunks=chunks, rows=rows, groups=g...]
    convert_element_type x8 -> x0, other arithmetic: 38 us -> none  [mix_rows(): mixed_real = (real_in * cosine + imag_in * sine_part).astype(jnp.bfloat16)]
  transfers between devices with their start and end apart: 3 -> 1, of which waited for: 3 -> 1; matrix products, arithmetic and copies ran while one was open for 0% -> 2% of each run, Pallas kernels for 0% -> 0%
where the time goes in v1:
time: 115 us; the launch traced here: 114 us
  waiting for transfers between devices  55.3 us (48%)
  Pallas kernels  40.8 us (35%)
  between operations  13.4 us (12%)
  local copies, waits for them, and re-layouts  3.27 us (3%)
  other arithmetic  1.42 us (1%)
    all_gather x1, waiting for transfers between devices, gather(): return lax.all_gather(value, ('tm', 'dop'), axis=0, tiled=False)  55.3 us
    pallas_call x1, Pallas kernels, on_device(): pl.pallas_call(functools.partial(body, chunks=chunks, rows=rows, groups=g...  40.8 us
  transfers between devices with their start and end apart: 1, of which 1 were waited for; matrix products, arithmetic and copies ran while one was open for 2% of the time, Pallas kernels for 0%

profile of v1, /device:TPU:0, one launch (start us, length us, event | category | flops | bytes accessed | tf_op | source)
XLA Modules:
  0.0 114.2 jit_solution(6236836428671886025)
XLA Ops:
  6.5 0.0 all-gather.3.cloned.1.call-start
  6.5 0.8 pad_maximum_fusion
  7.3 0.1 reshape.7
  7.5 0.1 copy.10
  7.6 0.2 rev.3
  7.8 0.1 copy.11
  7.9 0.6 pad_maximum_fusion.1
  8.5 0.0 all-gather.3.cloned.1.call-update
  8.5 1.4 %dynamic-slice_bitcast_fusion.mix_ref = f32[2,32,128]{2,1,0:T(8,128)} fusion(f32[2,2,32,128]{3,2,1,0:T(8,128)} %constant.33.clone, s32[]{:T(128)S(6)} %select_n.6), kind=kLoop, calls=%fused_computation.2 | loop fusion | bytes 65540 | tf_op jit(solution)/shard_map/jit(dynamic_index_in_dim)/squeeze | solution.py:151
  9.9 1.4 %constant_dynamic-slice_fusion = f32[1,2,32,1,128]{4,2,1,3,0:T(8,128)} fusion(f32[2,2,32,1,128]{4,2,1,3,0:T(8,128)} %constant.34.clone, s32[]{:T(128)S(6)} %select_n.6), kind=kLoop, calls=%fused_computation.3 | loop fusion | bytes 65540 | tf_op jit(solution)/shard_map/jit(dynamic_index_in_dim)/dynamic_slice | solution.py:152
  11.3 55.3 %all-gather.3.cloned.1.call-done = bf16[128,32,128]{2,1,0:T(8,128)(2,1)} async-done(((bf16[4,32,128]{2,1,0:T(8,128)(2,1)}), bf16[128,32,128]{2,1,0:T(8,128)(2,1)}) %all-gather.3.cloned.1.call-update) | async-done | bytes 1048592 | tf_op jit(solution)/shard_map/all_gather | solution.py:108
  66.6 40.8 %shard_map.73 = f32[128,2,256]{2,1,0:T(2,128)} custom-call(s32[1]{0:T(128)} %bitcast.pos_ref, bf16[32,4,32,128]{3,2,1,0:T(8,128)(2,1)} %bitcast.8, bf16[16,256,256]{2,1,0:T(8,128)(2,1)} %constant.31.clone.d_ref, f32[2,32,128]{2,1,0:T(8,128)} %dynamic-slice_bitcast_fusion.mix_ref, f32[2,32,1,128]{3,2,1,0:T(1,128)} %bitcast.10, ...), custom_call_target="tpu_custom_call" | custom-call | tf_op jit(solution)/shard_map/pallas_call | solution.py:156
  (1 shorter events, 0.0 us)
Async XLA Ops:
  6.5 60.0 %all-gather.3.cloned.1.call-start = ((), (), s32[]{:S(2)}) async-start(), calls=%async_computation | async-start | bytes 1081344 | tf_op jit(solution)/shard_map/all_gather | solution.py:108
Sparse Core Ops, SparseCore 0:
  10.2 56.3 all-gather.2

commit v2 on v1

--- a/solution.py
+++ b/solution.py
@@ -105,7 +105,8 @@
 
 
 def gather(value, tm, dop):
-    return lax.all_gather(value, ("tm", "dop"), axis=0, tiled=False)
+    copies = jnp.broadcast_to(value[None], (tm * dop,) + value.shape)
+    return lax.all_to_all(copies, ("tm", "dop"), 0, 0)
 
 
 def on_device(surveillance, reference_signal):

time: 115 us -> 78.2 us (0.68)
  waiting for transfers between devices: 55.3 us -> 25 us
  between operations: 13.4 us -> 0.06 us
  starting transfers between devices: 0.01 us -> 7.33 us
    all_gather x1 -> x0, waiting for transfers between devices: 55.3 us -> none  [gather(): return lax.all_gather(value, ('tm', 'dop'), axis=0, tiled=False)]
    all_to_all x0 -> x1, waiting for transfers between devices: none -> 25 us  [gather(): return lax.all_to_all(copies, ('tm', 'dop'), 0, 0)]
    all_to_all x0 -> x1, starting transfers between devices: none -> 7.33 us  [gather(): return lax.all_to_all(copies, ('tm', 'dop'), 0, 0)]
    broadcast_in_dim x0 -> x1, local copies, waits for them, and re-layouts: none -> 1.22 us  [gather(): copies = jnp.broadcast_to(value[None], (tm * dop,) + value.shape)]
where the time goes in v2:
time: 78.2 us; the launch traced here: 77.9 us
  Pallas kernels  40.8 us (52%)
  waiting for transfers between devices  25 us (32%)
  starting transfers between devices  7.33 us (9%)
  local copies, waits for them, and re-layouts  3.95 us (5%)
  other arithmetic  0.83 us (1%)
    pallas_call x1, Pallas kernels, on_device(): pl.pallas_call(functools.partial(body, chunks=chunks, rows=rows, groups=g...  40.8 us
    all_to_all x1, waiting for transfers between devices, gather(): return lax.all_to_all(copies, ('tm', 'dop'), 0, 0)  25 us
    all_to_all x1, starting transfers between devices, gather(): return lax.all_to_all(copies, ('tm', 'dop'), 0, 0)  7.33 us
  transfers between devices with their start and end apart: 1, of which 1 were waited for; matrix products, arithmetic and copies ran while one was open for 2% of the time, Pallas kernels for 0%

profile of v2, /device:TPU:0, one launch (start us, length us, event | category | flops | bytes accessed | tf_op | source)
XLA Modules:
  0.0 77.9 jit_solution(14596551448481445822)
XLA Ops:
  0.0 0.0 copy-start.2
  0.0 0.0 copy-start.1
  0.0 0.8 %pad_maximum_fusion = bf16[4,1,4096]{2,0,1:T(4,128)(2,1)S(1)} fusion(bf16[2,1,4096]{2,0,1:T(2,128)(2,1)} %param.8, bf16[2,1,4096]{2,0,1:T(2,128)(2,1)} %param.7), kind=kLoop, calls=%fused_computation | loop fusion | flops 65536 | bytes 65536 | tf_op jit(solution)/shard_map/concatenate | solution.py:127
  0.8 0.1 reshape.8
  1.0 0.2 rev.3
  1.2 0.1 copy.11
  1.3 0.1 copy.10
  1.4 1.2 %broadcast_in_dim.2 = bf16[32,4,32,128]{3,2,1,0:T(8,128)(2,1)} broadcast(bf16[4,32,128]{2,1,0:T(8,128)(2,1)S(1)} %pad_maximum_fusion.1), dimensions={1,2,3} | broadcast | bytes 1081344 | tf_op jit(solution)/shard_map/broadcast_in_dim | solution.py:108
  2.6 7.3 %all-to-all-start = ((bf16[32,4,32,128]{3,2,1,0:T(8,128)(2,1)}), bf16[32,4,32,128]{3,2,1,0:T(8,128)(2,1)S(1)}, u32[]{:S(2)}, u32[]{:S(2)}) async-start(bf16[32,4,32,128]{3,2,1,0:T(8,128)(2,1)} %broadcast_in_dim.2), calls=%async_computation | async-start | bytes 2097152 | tf_op jit(solution)/shard_map/all_to_all | solution.py:109
  10.0 0.0 copy-done.2
  10.0 0.6 dynamic-slice_bitcast_fusion.mix_ref
  10.6 0.0 copy-done.1
  10.6 0.6 constant_dynamic-slice_fusion
  11.2 25.0 %all-to-all-done.g_ref = bf16[32,4,32,128]{3,2,1,0:T(8,128)(2,1)S(1)} async-done(((bf16[32,4,32,128]{3,2,1,0:T(8,128)(2,1)}), bf16[32,4,32,128]{3,2,1,0:T(8,128)(2,1)S(1)}, u32[]{:S(2)}, u32[]{:S(2)}) %all-to-all-start) | async-done | bytes 1048608 | tf_op jit(solution)/shard_map/all_to_all | solution.py:109
  36.2 0.0 copy-start
  36.2 1.0 %copy-done = bf16[32,4,32,128]{3,2,1,0:T(8,128)(2,1)} copy-done((bf16[32,4,32,128]{3,2,1,0:T(8,128)(2,1)}, bf16[32,4,32,128]{3,2,1,0:T(8,128)(2,1)S(1)}, u32[]{:S(2)}) %copy-start) | copy-done | bytes 1048600
  37.1 40.8 %shard_map.73 = f32[128,2,256]{2,1,0:T(2,128)} custom-call(s32[1]{0:T(128)} %bitcast.pos_ref, bf16[32,4,32,128]{3,2,1,0:T(8,128)(2,1)} %copy-done, bf16[16,256,256]{2,1,0:T(8,128)(2,1)} %constant.31.clone.d_ref, f32[2,32,128]{2,1,0:T(8,128)} %dynamic-slice_bitcast_fusion.mix_ref, f32[2,32,1,128]{3,2,1,0:T(1,128)} %bitcast.8, ...), custom_call_target="tpu_custom_call" | custom-call | tf_op jit(solution)/shard_map/pallas_call | solution.py:157
  (2 shorter events, 0.0 us)
Async XLA Ops:
  0.0 10.0 %copy-start.2 = (f32[2,2,32,128]{3,2,1,0:T(8,128)S(1)}, f32[2,2,32,128]{3,2,1,0:T(8,128)}, u32[]{:S(2)}) copy-start(f32[2,2,32,128]{3,2,1,0:T(8,128)} %constant.33.clone) | copy-start | bytes 196612
  0.0 10.6 %copy-start.1 = (f32[2,2,32,1,128]{4,2,1,3,0:T(8,128)S(1)}, f32[2,2,32,1,128]{4,2,1,3,0:T(8,128)}, u32[]{:S(2)}) copy-start(f32[2,2,32,1,128]{4,2,1,3,0:T(8,128)} %constant.34.clone) | copy-start | bytes 196612
  2.6 33.5 %all-to-all-start = ((bf16[32,4,32,128]{3,2,1,0:T(8,128)(2,1)}), bf16[32,4,32,128]{3,2,1,0:T(8,128)(2,1)S(1)}, u32[]{:S(2)}, u32[]{:S(2)}) async-start(bf16[32,4,32,128]{3,2,1,0:T(8,128)(2,1)} %broadcast_in_dim.2), calls=%async_computation | async-start | bytes 2097152 | tf_op jit(solution)/shard_map/all_to_all | solution.py:109
  36.2 1.0 %copy-start = (bf16[32,4,32,128]{3,2,1,0:T(8,128)(2,1)}, bf16[32,4,32,128]{3,2,1,0:T(8,128)(2,1)S(1)}, u32[]{:S(2)}) copy-start(bf16[32,4,32,128]{3,2,1,0:T(8,128)(2,1)S(1)} %all-to-all-done.g_ref) | copy-start | bytes 3145732
